TPU v7x, 32 devices: a whole 2x2x4 slice. The times are simulated.
32 devices in a mesh: tm: 8 (over y, x, core), chan: 4 (over z).
Axes of the slice: x: 2, y: 2, z: 4, core: 2. Of those that a mesh axis runs over, the one named last changes fastest.
Arguments:
- inputs: bfloat16 [4096, 8192], P('tm', 'chan'), may hold values from -52 to 52
- gate_logits: bfloat16 [4096, 8192], P(('tm', 'chan')), may hold values from -5 to 5
- step_sizes: bfloat16 [4096, 64], P('tm', 'chan'), may hold values from 0.3 to 28672, as said below
- decay_rates: float32 [8192], replicated, as said below
- skip_gain: float32 [8192], replicated, may hold values from 0.3 to 0.8
- norm_gain: float32 [8192], replicated, may hold values from 0.25 to 1.75
Outputs:
- outputs: bfloat16 [4096, 8192], P(('tm', 'chan'))
Inputs may be any that keep to these rules, and one draw needn't show every extreme that they name: `step_sizes`: every step size is positive. `decay_rates`: every rate is positive.
All inputs are finite; a program needn't handle non-finite values.
Results may differ from a plain program's by a relative error of at most 0.0049.
Values may be sent and summed in bfloat16 or wider, within the bound.
A program may use at most 64 MiB of HBM per device.

v0:
```python
import jax
import jax.numpy as jnp
from jax import lax
from jax.sharding import PartitionSpec as P

norm_epsilon = 1e-05


def entering(value, axis, combine, identity):
    count, mine = (lax.axis_size(axis), lax.axis_index(axis))
    everything = jax.tree.map(lambda part: lax.all_gather(part, axis), value)
    start = jax.tree.map(
        lambda part, zero: jnp.broadcast_to(jnp.asarray(zero, part.dtype), part.shape),
        value,
        identity,
    )

    def turn(k, before):
        reached = k < mine
        new = combine(before, jax.tree.map(lambda part: part[k], everything))
        return jax.tree.map(lambda a, b: jnp.where(reached, a, b), new, before)

    return lax.fori_loop(0, count, turn, start)


def combine_pairs(earlier, later):
    return (earlier[0] * later[0], later[0] * earlier[1] + later[1])


def widen(head_values, channels):
    head_count = head_values.shape[1]
    width_each = channels // head_count
    owner = lax.broadcasted_iota(jnp.int32, (head_count, channels), 1) // width_each
    column_head = lax.broadcasted_iota(jnp.int32, (head_count, channels), 0)
    spread_table = (owner == column_head).astype(jnp.float32)
    return jnp.dot(
        head_values,
        spread_table,
        precision=lax.Precision.HIGHEST,
        preferred_element_type=jnp.float32,
    )


def serial_rows(decays, drives, axis_pos):
    length = decays.shape[axis_pos]
    prod_list = []
    state_list = []
    prod_now = None
    state_now = None
    for index in range(length):
        decay_here = lax.index_in_dim(decays, index, axis_pos, keepdims=False)
        drive_here = lax.index_in_dim(drives, index, axis_pos, keepdims=False)
        if index == 0:
            prod_now = decay_here
            state_now = drive_here
        else:
            prod_now = prod_now * decay_here
            state_now = decay_here * state_now + drive_here
        prod_list.append(prod_now)
        state_list.append(state_now)
    return (jnp.stack(prod_list, axis=axis_pos), jnp.stack(state_list, axis=axis_pos))


def prefix_rows(decays, drives):
    length = decays.shape[0]
    channels = decays.shape[1]
    if length <= 8:
        return serial_rows(decays, drives, 0)
    group = 8
    groups = length // group
    grouped_decay = decays.reshape(groups, group, channels)
    grouped_drive = drives.reshape(groups, group, channels)
    inner_prod, inner_state = serial_rows(grouped_decay, grouped_drive, 1)
    outer_prod, outer_state = prefix_rows(inner_prod[:, -1, :], inner_state[:, -1, :])
    before_prod = jnp.concatenate([jnp.ones((1, channels), jnp.float32), outer_prod[:-1]], axis=0)
    before_state = jnp.concatenate(
        [jnp.zeros((1, channels), jnp.float32), outer_state[:-1]], axis=0
    )
    products = inner_prod * before_prod[:, None, :]
    states = inner_state + inner_prod * before_state[:, None, :]
    return (products.reshape(length, channels), states.reshape(length, channels))


def chain_time(end_decay, end_state):
    identity = (jnp.ones_like(end_decay), jnp.zeros_like(end_state))
    return entering((end_decay, end_state), "tm", combine_pairs, identity)[1]


def recurrence(block_inputs, block_steps, rates_here, skip_here, chain_fn):
    channels = block_inputs.shape[1]
    step_values = block_steps.astype(jnp.float32)
    widened = widen(step_values, channels) * rates_here[None, :]
    decays = jnp.exp(-widened)
    values = block_inputs.astype(jnp.float32)
    drives = jnp.sqrt(-jnp.expm1(-2.0 * widened)) * values
    products, local_states = prefix_rows(decays, drives)
    incoming = chain_fn(products[-1], local_states[-1])
    states = local_states + products * incoming[None, :]
    return (states + skip_here[None, :] * values).astype(jnp.bfloat16)


def normalize(mixed_rows, gate_logits, norm_gain):
    gated = mixed_rows.astype(jnp.float32) * jax.nn.silu(gate_logits.astype(jnp.float32))
    factor = lax.rsqrt(jnp.mean(gated * gated, axis=1, keepdims=True) + norm_epsilon)
    return (gated * factor * norm_gain[None, :]).astype(jnp.bfloat16)


def per_device(inputs, gate_logits, step_sizes, decay_rates, skip_gain, norm_gain):
    channels = inputs.shape[1]
    offset = lax.axis_index("chan") * channels
    rates_here = lax.dynamic_slice_in_dim(decay_rates, offset, channels, 0)
    skip_here = lax.dynamic_slice_in_dim(skip_gain, offset, channels, 0)
    mixed_rows = recurrence(inputs, step_sizes, rates_here, skip_here, chain_time)
    framed = lax.all_to_all(mixed_rows, "chan", split_axis=0, concat_axis=1, tiled=True)
    return normalize(framed, gate_logits, norm_gain)


def solution(mesh):
    in_specs = (P("tm", "chan"), P(("tm", "chan"), None), P("tm", "chan"), P(), P(), P())
    out_specs = P(("tm", "chan"), None)
    return jax.shard_map(
        per_device, mesh=mesh, in_specs=in_specs, out_specs=out_specs, check_vma=False
    )
```

profile of v0, /device:TPU:0, one launch (start us, length us, event | category | flops | bytes accessed | tf_op | source)
XLA Modules:
  0.0 148.7 jit_solution(7240075363780846964)
XLA Ops:
  0.0 0.0 copy-start
  0.0 0.7 dynamic_slice.20
  0.7 0.0 copy-done
  0.7 0.7 fusion.7
  1.5 0.0 copy-start.4
  1.5 0.9 exponential_bitcast_fusion
  2.4 0.6 copy-done.4
  3.1 2.7 %fusion = f32[64,8,2048]{2,1,0:T(8,128)S(1)} fusion(bf16[512,2048]{1,0:T(8,128)(2,1)S(1)} %copy-done.4, f32[2048,512]{0,1:T(8,128)S(1)} %fusion.7, f32[2048]{0:T(1024)S(1)} %dynamic_slice.20), kind=kLoop, calls=%fused_computation.7 | loop fusion | flops 5242880 | bytes 10493952 | tf_op jit(solution)/shard_map/reshape | solution.py:72
  5.8 6.3 %slice_multiply_fusion = (f32[64,1,2048]{2,1,0:T(1,128)S(1)}, f32[64,1,2048]{2,1,0:T(1,128)}, f32[64,1,2048]{2,1,0:T(1,128)}, f32[64,1,2048]{2,1,0:T(1,128)}, f3...) fusion(f32[64,8,2048]{2,1,0:T(8,128)S(1)} %exponential_bitcast_fusion), kind=kLoop, calls=%fused_computation.31 | loop fusion | flops 917504 | bytes 8388608 | tf_op jit(solution)/shard_map/mul | solution.py:57
  12.0 8.5 %slice_add_fusion = (f32[64,1,2048]{2,1,0:T(1,128)S(1)}, f32[64,1,2048]{2,1,0:T(1,128)}, f32[64,1,2048]{2,1,0:T(1,128)}, f32[64,1,2048]{2,1,0:T(1,128)}, f32[64,...) fusion(f32[64,8,2048]{2,1,0:T(8,128)S(1)} %fusion, ...), kind=kLoop, calls=%fused_computation.20 | loop fusion | flops 1835008 | bytes 12058624 | tf_op jit(solution)/shard_map/add | solution.py:58
  20.6 0.2 copy.19
  20.8 0.2 copy.18
  20.9 1.1 slice_multiply_fusion.7
  22.0 1.4 slice_add_fusion.7
  23.4 0.6 slice_bitcast_fusion.15
  24.0 0.1 fusion.13
  24.1 0.7 fusion.25
  24.8 2.3 %stack.10 = f32[8,8,2048]{2,1,0:T(8,128)} concatenate(f32[8,1,2048]{2,1,0:T(1,128)} %get-tuple-element.177, f32[8,1,2048]{2,1,0:T(1,128)} %get-tuple-element.153, f32[8,1,2048]{2,1,0:T(1,128)} %get-tuple-element.152, f32[8,1,2048]{2,1,0:T(1,128)} %get-tuple-element.151, f32[8,1,2048]{2,1,0:T(1,128)} %get-tuple-element.150, f32[8,1,2048]{2,1,0:T(1,128)} %get-tuple-element.149, ...), dimensions={1} | concatenate | bytes 1048576 | tf_op jit(solution)/shard_map/stack | solution.py:61
  27.1 2.2 %stack.11 = f32[8,8,2048]{2,1,0:T(8,128)} concatenate(f32[8,1,2048]{2,1,0:T(1,128)} %get-tuple-element.176, f32[8,1,2048]{2,1,0:T(1,128)} %get-tuple-element.146, f32[8,1,2048]{2,1,0:T(1,128)} %get-tuple-element.145, f32[8,1,2048]{2,1,0:T(1,128)} %get-tuple-element.144, f32[8,1,2048]{2,1,0:T(1,128)S(1)} %get-tuple-element.143, f32[8,1,2048]{2,1,0:T(1,128)S(1)} %get-tuple-element.142, ...), dimensions={1} | concatenate | bytes 1048576 | tf_op jit(solution)/shard_map/stack | solution.py:61
  29.3 0.8 concatenate.12
  30.1 0.9 concatenate.14
  31.0 1.3 multiply_bitcast_fusion.1
  32.3 0.8 concatenate.13
  33.1 0.8 concatenate.15
  34.0 11.9 %stack.8 = f32[64,8,2048]{2,1,0:T(8,128)} concatenate(f32[64,1,2048]{2,1,0:T(1,128)} %get-tuple-element.173, f32[64,1,2048]{2,1,0:T(1,128)} %get-tuple-element.167, f32[64,1,2048]{2,1,0:T(1,128)} %get-tuple-element.166, f32[64,1,2048]{2,1,0:T(1,128)} %get-tuple-element.165, f32[64,1,2048]{2,1,0:T(1,128)} %get-tuple-element.164, f32[64,1,2048]{2,1,0:T(1,128)} %get-tuple-element.163, ...), dimensions={1} | concatenate | bytes 8388608 | tf_op jit(solution)/shard_map/stack | solution.py:61
  45.9 0.0 copy-start.5
  45.9 12.0 %stack.9 = f32[64,8,2048]{2,1,0:T(8,128)} concatenate(f32[64,1,2048]{2,1,0:T(1,128)} %get-tuple-element.172, f32[64,1,2048]{2,1,0:T(1,128)} %get-tuple-element.160, f32[64,1,2048]{2,1,0:T(1,128)} %get-tuple-element.159, f32[64,1,2048]{2,1,0:T(1,128)} %get-tuple-element.158, f32[64,1,2048]{2,1,0:T(1,128)} %get-tuple-element.157, f32[64,1,2048]{2,1,0:T(1,128)} %get-tuple-element.156, ...), dimensions={1} | concatenate | bytes 8388608 | tf_op jit(solution)/shard_map/stack | solution.py:61
  57.8 0.0 copy-done.5
  57.8 0.0 dynamic-slice-start
  57.8 5.6 %multiply_bitcast_fusion = (f32[512,2048]{1,0:T(8,128)S(1)}, f32[512,2048]{1,0:T(8,128)S(1)}) fusion(f32[64,8,2048]{2,1,0:T(8,128)} %stack.9, f32[64,2048]{1,0:T(8,128)} %concatenate.15, f32[64,8,2048]{2,1,0:T(8,128)} %stack.8, f32[64,2048]{1,0:T(8,128)S(1)} %copy-done.5), kind=kLoop, calls=%fused_computation.17 | loop fusion | flops 3145728 | bytes 17825792 | tf_op jit(solution)/shard_map/mul | solution.py:79
  63.5 0.0 copy-start.1
  63.5 0.0 copy-start.2
  63.5 10.7 %all-gather.1 = f32[8,1,2048]{2,1,0:T(1,128)S(1)} all-gather(f32[1,1,2048]{2,1,0:T(1,128)S(1)} %slice_bitcast_fusion), channel_id=1, replica_groups=mesh['tm'=8,'chan'=4] {'tm'}, dimensions={0}, use_global_device_ids=true | all-gather | bytes 73728 | tf_op jit(solution)/shard_map/all_gather | solution.py:11
  74.3 0.0 copy-done.1
  74.3 0.0 copy-done.2
  74.3 9.2 %all-gather = f32[8,1,2048]{2,1,0:T(1,128)S(1)} all-gather(f32[1,1,2048]{2,1,0:T(1,128)S(1)} %slice_bitcast_fusion.1), channel_id=1, replica_groups=mesh['tm'=8,'chan'=4] {'tm'}, dimensions={0}, use_global_device_ids=true | all-gather | bytes 73728 | tf_op jit(solution)/shard_map/all_gather | solution.py:11
  83.6 0.7 while.14
  84.3 0.0 dynamic-slice-done
  84.3 4.7 %fusion.2 = bf16[512,2048]{1,0:T(8,128)(2,1)S(1)} fusion(bf16[512,2048]{1,0:T(8,128)(2,1)S(1)} %copy-done.4, f32[512,2048]{1,0:T(8,128)} %copy-done.2, f32[512,2048]{1,0:T(8,128)} %copy-done.1, f32[2048]{0:T(1024)S(1)} %dynamic-slice-done, f32[2048]{0:T(1024)S(1)} %get-tuple-element.99), kind=kLoop, calls=%fused_computation.9 | loop fusion | flops 6291456 | bytes 12599296 | tf_op jit(solution)/shard_map/convert_element_type | solution.py:99
  89.0 53.4 %all_to_all.13 = bf16[4,128,2048]{2,1,0:T(8,128)(2,1)S(1)} all-to-all(bf16[4,128,2048]{2,1,0:T(8,128)(2,1)S(1)} %bitcast.133), channel_id=1, replica_groups=mesh['tm'=8,'chan'=4] {'chan'}, dimensions={0} | all-to-all | bytes 4194304 | tf_op jit(solution)/shard_map/all_to_all | solution.py:114
  142.4 0.5 convert_bitcast_fusion
  142.9 0.0 copy-start.3
  142.9 0.3 copy.13
  143.2 0.0 copy-start.6
  143.2 1.3 copy-done.3
  144.5 1.5 multiply_reduce_fusion
  145.9 0.0 copy-done.6
  146.0 2.8 %multiply_convert_fusion = bf16[128,8192]{1,0:T(8,128)(2,1)} fusion(f32[8192]{0:T(1024)S(1)} %copy-done.6, f32[128]{0:T(128)S(1)} %add_rsqrt_fusion, f32[128,8192]{1,0:T(8,128)S(1)} %bitcast.132, bf16[128,8192]{1,0:T(8,128)(2,1)S(1)} %copy-done.3), kind=kLoop, calls=%fused_computation.15 | loop fusion | flops 9437184 | bytes 8421888 | tf_op jit(solution)/shard_map/convert_element_type | solution.py:105
  (27 shorter events, 0.3 us)
Async XLA Ops:
  0.0 0.7 copy-start
  1.5 1.6 %copy-start.4 = (bf16[512,2048]{1,0:T(8,128)(2,1)S(1)}, bf16[512,2048]{1,0:T(8,128)(2,1)}, u32[]{:S(2)}) copy-start(bf16[512,2048]{1,0:T(8,128)(2,1)} %param.8) | copy-start | bytes 6291460
  45.9 12.0 %copy-start.5 = (f32[64,2048]{1,0:T(8,128)S(1)}, f32[64,2048]{1,0:T(8,128)}, u32[]{:S(2)}) copy-start(f32[64,2048]{1,0:T(8,128)} %concatenate.13) | copy-start | bytes 1572868
  57.8 26.5 %dynamic-slice-start = ((f32[8192]{0:T(1024)}, s32[]{:T(128)}), f32[2048]{0:T(1024)S(1)}, s32[]{:S(2)}) async-start(f32[8192]{0:T(1024)} %param.12, s32[]{:T(128)} %select_n.32), calls=%async_computation.1 | async-start | bytes 16896 | tf_op jit(solution)/shard_map/dynamic_slice | solution.py:112
  63.5 10.8 %copy-start.1 = (f32[512,2048]{1,0:T(8,128)}, f32[512,2048]{1,0:T(8,128)S(1)}, u32[]{:S(2)}) copy-start(f32[512,2048]{1,0:T(8,128)S(1)} %get-tuple-element.170) | copy-start | bytes 12582916
  63.5 10.8 %copy-start.2 = (f32[512,2048]{1,0:T(8,128)}, f32[512,2048]{1,0:T(8,128)S(1)}, u32[]{:S(2)}) copy-start(f32[512,2048]{1,0:T(8,128)S(1)} %get-tuple-element.171) | copy-start | bytes 12582916
  142.9 1.6 %copy-start.3 = (bf16[128,8192]{1,0:T(8,128)(2,1)S(1)}, bf16[128,8192]{1,0:T(8,128)(2,1)}, u32[]{:S(2)}) copy-start(bf16[128,8192]{1,0:T(8,128)(2,1)} %param.9) | copy-start | bytes 6291460
  143.2 2.8 %copy-start.6 = (f32[8192]{0:T(1024)S(1)}, f32[8192]{0:T(1024)}, u32[]{:S(2)}) copy-start(f32[8192]{0:T(1024)} %param.13) | copy-start | bytes 98308
where the time goes:
time: 152 us; the launch traced here: 149 us
  blocking collectives  73.3 us (48%)
  other arithmetic  38.1 us (25%)
  local copies, waits for them, and re-layouts  35.8 us (24%)
    all_to_all x1, blocking collectives, per_device(): lax.all_to_all(mixed_rows, 'chan', split_axis=0, concat_axis=1, tiled=True)  53.4 us
    all_gather x2, blocking collectives, entering(): everything = jax.tree.map(lambda part: lax.all_gather(part, axis), value)  20 us
    another operation x2, local copies, waits for them, and re-layouts, serial_rows(): jnp.stack(prod_list, axis=axis_pos)  14.2 us
    another operation x2, local copies, waits for them, and re-layouts, serial_rows(): jnp.stack(state_list, axis=axis_pos)  14.2 us
    add x3, other arithmetic, serial_rows(): state_now = decay_here * state_now + drive_here  10 us
    mul x3, other arithmetic, serial_rows(): prod_now = prod_now * decay_here  8 us
    mul x2, other arithmetic, prefix_rows(): products = inner_prod * before_prod[:, None, :]  6.93 us
    convert_element_type x1, other arithmetic, recurrence(): return (states + skip_here[None, :] * values).astype(jnp.bfloat16)  4.67 us

commit v1 on v0

--- a/solution.py
+++ b/solution.py
@@ -111,7 +111,12 @@
     rates_here = lax.dynamic_slice_in_dim(decay_rates, offset, channels, 0)
     skip_here = lax.dynamic_slice_in_dim(skip_gain, offset, channels, 0)
     mixed_rows = recurrence(inputs, step_sizes, rates_here, skip_here, chain_time)
-    framed = lax.all_to_all(mixed_rows, "chan", split_axis=0, concat_axis=1, tiled=True)
+    framed = jnp.concatenate(
+        lax.all_to_all(
+            jnp.stack(jnp.split(mixed_rows, lax.axis_size("chan"), axis=0)), "chan", 0, 0
+        ),
+        axis=1,
+    )
     return normalize(framed, gate_logits, norm_gain)
 
 

time: 152 us -> 168 us (1.11)
  blocking collectives: 73.3 us -> 20 us
  waiting for transfers between devices: 0 us -> 45.6 us
  local copies, waits for them, and re-layouts: 35.8 us -> 45.8 us
  other arithmetic: 38.1 us -> 47.3 us
  starting transfers between devices: 0 us -> 4.87 us
    all_to_all x1 -> x0, blocking collectives: 53.4 us -> none  [per_device(): lax.all_to_all(mixed_rows, 'chan', split_axis=0, concat_axis=1, tiled=True)]
    all_to_all x0 -> x1, waiting for transfers between devices: none -> 45.6 us  [per_device(): lax.all_to_all(jnp.stack(jnp.split(mixed_rows, lax.axis_size('chan'), axi...]
    convert_element_type x1, local copies, waits for them, and re-layouts: 0.27 us -> 5.37 us  [normalize(): mixed_rows.astype(jnp.float32)]
    all_to_all x0 -> x1, starting transfers between devices: none -> 4.87 us  [per_device(): lax.all_to_all(jnp.stack(jnp.split(mixed_rows, lax.axis_size('chan'), axi...]
    convert_element_type x0 -> x1, local copies, waits for them, and re-layouts: none -> 4.06 us  [normalize(): return (gated * factor * norm_gain[None, :]).astype(jnp.bfloat16)]
    convert_element_type x0 -> x1, other arithmetic: none -> 4.06 us  [normalize(): mixed_rows.astype(jnp.float32)]
    reduce_sum x1, other arithmetic: 1.45 us -> 3.78 us  [normalize(): jnp.mean(gated * gated, axis=1, keepdims=True) + norm_epsilon]
    unnamed x20 -> x23, local copies, waits for them, and re-layouts: 2.35 us -> 4.28 us
  transfers between devices with their start and end apart: 0 -> 1, of which waited for: 0 -> 1; matrix products, arithmetic and copies ran while one was open for 0% -> 2% of each run, Pallas kernels for 0% -> 0%
where the time goes in v1:
time: 168 us; the launch traced here: 165 us
  other arithmetic  47.3 us (28%)
  local copies, waits for them, and re-layouts  45.8 us (27%)
  waiting for transfers between devices  45.6 us (27%)
  blocking collectives  20 us (12%)
  starting transfers between devices  4.87 us (3%)
    all_to_all x1, waiting for transfers between devices, per_device(): lax.all_to_all(jnp.stack(jnp.split(mixed_rows, lax.axis_size('chan'), axi...  45.6 us
    all_gather x2, blocking collectives, entering(): everything = jax.tree.map(lambda part: lax.all_gather(part, axis), value)  20 us
    another operation x2, local copies, waits for them, and re-layouts, serial_rows(): jnp.stack(prod_list, axis=axis_pos)  14.2 us
    another operation x2, local copies, waits for them, and re-layouts, serial_rows(): jnp.stack(state_list, axis=axis_pos)  14.2 us
    add x3, other arithmetic, serial_rows(): state_now = decay_here * state_now + drive_here  10 us
    mul x3, other arithmetic, serial_rows(): prod_now = prod_now * decay_here  7.97 us
    mul x2, other arithmetic, prefix_rows(): products = inner_prod * before_prod[:, None, :]  6.93 us
    convert_element_type x1, local copies, waits for them, and re-layouts, normalize(): mixed_rows.astype(jnp.float32)  5.37 us
  transfers between devices with their start and end apart: 1, of which 1 were waited for; matrix products, arithmetic and copies ran while one was open for 2% of the time, Pallas kernels for 0%

profile of v1, /device:TPU:0, one launch (start us, length us, event | category | flops | bytes accessed | tf_op | source)
XLA Modules:
  0.0 164.9 jit_solution(15479669842930217423)
XLA Ops:
  0.0 0.0 copy-start
  0.0 0.7 dynamic_slice.20
  0.7 0.0 copy-done
  0.7 0.7 fusion.7
  1.5 0.0 copy-start.5
  1.5 0.9 exponential_bitcast_fusion
  2.4 0.6 copy-done.5
  3.1 2.7 %fusion = f32[64,8,2048]{2,1,0:T(8,128)S(1)} fusion(bf16[512,2048]{1,0:T(8,128)(2,1)S(1)} %copy-done.5, f32[2048,512]{0,1:T(8,128)S(1)} %fusion.7, f32[2048]{0:T(1024)S(1)} %dynamic_slice.20), kind=kLoop, calls=%fused_computation.7 | loop fusion | flops 5242880 | bytes 10493952 | tf_op jit(solution)/shard_map/reshape | solution.py:72
  5.8 6.3 %slice_multiply_fusion = (f32[64,1,2048]{2,1,0:T(1,128)S(1)}, f32[64,1,2048]{2,1,0:T(1,128)}, f32[64,1,2048]{2,1,0:T(1,128)}, f32[64,1,2048]{2,1,0:T(1,128)}, f3...) fusion(f32[64,8,2048]{2,1,0:T(8,128)S(1)} %exponential_bitcast_fusion), kind=kLoop, calls=%fused_computation.36 | loop fusion | flops 917504 | bytes 8388608 | tf_op jit(solution)/shard_map/mul | solution.py:57
  12.0 8.5 %slice_add_fusion = (f32[64,1,2048]{2,1,0:T(1,128)S(1)}, f32[64,1,2048]{2,1,0:T(1,128)}, f32[64,1,2048]{2,1,0:T(1,128)}, f32[64,1,2048]{2,1,0:T(1,128)}, f32[64,...) fusion(f32[64,8,2048]{2,1,0:T(8,128)S(1)} %fusion, ...), kind=kLoop, calls=%fused_computation.25 | loop fusion | flops 1835008 | bytes 12058624 | tf_op jit(solution)/shard_map/add | solution.py:58
  20.6 0.2 copy.22
  20.8 0.2 copy.21
  20.9 1.1 slice_multiply_fusion.7
  22.0 1.4 slice_add_fusion.7
  23.4 0.1 fusion.13
  23.5 0.6 fusion.25
  24.1 2.3 %stack.20 = f32[8,8,2048]{2,1,0:T(8,128)} concatenate(f32[8,1,2048]{2,1,0:T(1,128)} %get-tuple-element.181, f32[8,1,2048]{2,1,0:T(1,128)} %get-tuple-element.153, f32[8,1,2048]{2,1,0:T(1,128)} %get-tuple-element.152, f32[8,1,2048]{2,1,0:T(1,128)} %get-tuple-element.151, f32[8,1,2048]{2,1,0:T(1,128)} %get-tuple-element.150, f32[8,1,2048]{2,1,0:T(1,128)} %get-tuple-element.149, ...), dimensions={1} | concatenate | bytes 1048576 | tf_op jit(solution)/shard_map/stack | solution.py:61
  26.4 2.2 %stack.21 = f32[8,8,2048]{2,1,0:T(8,128)} concatenate(f32[8,1,2048]{2,1,0:T(1,128)} %get-tuple-element.180, f32[8,1,2048]{2,1,0:T(1,128)} %get-tuple-element.146, f32[8,1,2048]{2,1,0:T(1,128)} %get-tuple-element.145, f32[8,1,2048]{2,1,0:T(1,128)} %get-tuple-element.144, f32[8,1,2048]{2,1,0:T(1,128)S(1)} %get-tuple-element.143, f32[8,1,2048]{2,1,0:T(1,128)S(1)} %get-tuple-element.142, ...), dimensions={1} | concatenate | bytes 1048576 | tf_op jit(solution)/shard_map/stack | solution.py:61
  28.7 0.1 concatenate.12
  28.8 0.9 concatenate.14
  29.7 1.3 multiply_bitcast_fusion.1
  31.0 0.9 concatenate.13
  31.8 0.8 concatenate.15
  32.7 11.9 %stack.18 = f32[64,8,2048]{2,1,0:T(8,128)} concatenate(f32[64,1,2048]{2,1,0:T(1,128)} %get-tuple-element.173, f32[64,1,2048]{2,1,0:T(1,128)} %get-tuple-element.167, f32[64,1,2048]{2,1,0:T(1,128)} %get-tuple-element.166, f32[64,1,2048]{2,1,0:T(1,128)} %get-tuple-element.165, f32[64,1,2048]{2,1,0:T(1,128)} %get-tuple-element.164, f32[64,1,2048]{2,1,0:T(1,128)} %get-tuple-element.163, ...), dimensions={1} | concatenate | bytes 8388608 | tf_op jit(solution)/shard_map/stack | solution.py:61
  44.5 12.0 %stack.19 = f32[64,8,2048]{2,1,0:T(8,128)} concatenate(f32[64,1,2048]{2,1,0:T(1,128)} %get-tuple-element.172, f32[64,1,2048]{2,1,0:T(1,128)} %get-tuple-element.160, f32[64,1,2048]{2,1,0:T(1,128)} %get-tuple-element.159, f32[64,1,2048]{2,1,0:T(1,128)} %get-tuple-element.158, f32[64,1,2048]{2,1,0:T(1,128)} %get-tuple-element.157, f32[64,1,2048]{2,1,0:T(1,128)} %get-tuple-element.156, ...), dimensions={1} | concatenate | bytes 8388608 | tf_op jit(solution)/shard_map/stack | solution.py:61
  56.5 0.0 copy-done.6
  56.5 0.0 dynamic-slice-start
  56.6 5.6 %multiply_bitcast_fusion = (f32[512,2048]{1,0:T(8,128)S(1)}, f32[512,2048]{1,0:T(8,128)S(1)}) fusion(f32[64,8,2048]{2,1,0:T(8,128)} %stack.19, f32[64,2048]{1,0:T(8,128)} %concatenate.15, f32[64,8,2048]{2,1,0:T(8,128)} %stack.18, f32[64,2048]{1,0:T(8,128)S(1)} %copy-done.6), kind=kLoop, calls=%fused_computation.17 | loop fusion | flops 3145728 | bytes 17825792 | tf_op jit(solution)/shard_map/mul | solution.py:79
  62.2 0.0 copy-start.3
  62.2 0.0 copy-start.4
  62.2 10.7 %all-gather.1 = f32[8,1,2048]{2,1,0:T(1,128)S(1)} all-gather(f32[1,1,2048]{2,1,0:T(1,128)S(1)} %slice_bitcast_fusion.4), channel_id=1, replica_groups=mesh['tm'=8,'chan'=4] {'tm'}, dimensions={0}, use_global_device_ids=true | all-gather | bytes 73728 | tf_op jit(solution)/shard_map/all_gather | solution.py:11
  73.0 0.0 copy-done.3
  73.0 0.0 copy-done.4
  73.0 9.2 %all-gather = f32[8,1,2048]{2,1,0:T(1,128)S(1)} all-gather(f32[1,1,2048]{2,1,0:T(1,128)S(1)} %slice_bitcast_fusion.5), channel_id=1, replica_groups=mesh['tm'=8,'chan'=4] {'tm'}, dimensions={0}, use_global_device_ids=true | all-gather | bytes 73728 | tf_op jit(solution)/shard_map/all_gather | solution.py:11
  82.3 0.7 while.14
  83.0 0.0 dynamic-slice-done
  83.0 4.7 %fusion.2 = bf16[512,2048]{1,0:T(8,128)(2,1)S(1)} fusion(bf16[512,2048]{1,0:T(8,128)(2,1)S(1)} %copy-done.5, f32[512,2048]{1,0:T(8,128)} %copy-done.4, f32[512,2048]{1,0:T(8,128)} %copy-done.3, f32[2048]{0:T(1024)S(1)} %dynamic-slice-done, f32[2048]{0:T(1024)S(1)} %get-tuple-element.99), kind=kLoop, calls=%fused_computation.9 | loop fusion | flops 6291456 | bytes 12599296 | tf_op jit(solution)/shard_map/convert_element_type | solution.py:99
  87.7 0.1 slice_bitcast_fusion.3
  87.8 1.6 pad_maximum_fusion
  89.4 4.9 %all-to-all-start = ((bf16[4,128,2048]{2,1,0:T(8,128)(2,1)}), bf16[4,128,2048]{2,1,0:T(8,128)(2,1)}, u32[]{:S(2)}, u32[]{:S(2)}) async-start(bf16[4,128,2048]{2,1,0:T(8,128)(2,1)} %pad_maximum_fusion), calls=%async_computation | async-start | bytes 4194304 | tf_op jit(solution)/shard_map/all_to_all | solution.py:115
  94.3 3.2 %copy.11 = bf16[128,8192]{0,1:T(8,128)(2,1)S(1)} copy(bf16[128,8192]{1,0:T(8,128)(2,1)} %param.9) | data formatting | bytes 4194304 | tf_op args[1]
  97.5 45.6 %all-to-all-done = bf16[4,128,2048]{2,1,0:T(8,128)(2,1)} async-done(((bf16[4,128,2048]{2,1,0:T(8,128)(2,1)}), bf16[4,128,2048]{2,1,0:T(8,128)(2,1)}, u32[]{:S(2)}, u32[]{:S(2)}) %all-to-all-start) | async-done | bytes 2097184 | tf_op jit(solution)/shard_map/all_to_all | solution.py:115
  143.1 4.1 %convert_bitcast_fusion = f32[128,4,2048]{2,0,1:T(8,128)} fusion(bf16[4,128,2048]{2,1,0:T(8,128)(2,1)} %all-to-all-done), kind=kLoop, calls=%fused_computation.14 | loop fusion | flops 1048576 | bytes 6291456 | tf_op jit(solution)/shard_map/convert_element_type | solution.py:103
  147.2 5.4 %copy.10 = f32[128,4,2048]{0,2,1:T(8,128)} copy(f32[128,4,2048]{2,0,1:T(8,128)} %convert_bitcast_fusion) | data formatting | bytes 8388608 | tf_op jit(solution)/shard_map/convert_element_type | solution.py:103
  152.5 3.8 %multiply_reduce_fusion = f32[128]{0:T(128)S(1)} fusion(bf16[128,8192]{0,1:T(8,128)(2,1)S(1)} %copy.11, f32[128,4,2048]{0,2,1:T(8,128)} %copy.10), kind=kLoop, calls=%fused_computation.16 | loop fusion | flops 8388480 | bytes 6291968 | tf_op jit(solution)/shard_map/reduce_sum | solution.py:104
  156.3 0.0 copy-start.1
  156.4 4.5 %multiply_convert_fusion = bf16[128,8192]{0,1:T(8,128)(2,1)} fusion(f32[8192]{0:T(1024)S(1)} %copy-done.7, f32[128]{0:T(128)S(1)} %add_rsqrt_fusion, bf16[128,8192]{0,1:T(8,128)(2,1)S(1)} %copy.11, f32[128,4,2048]{0,2,1:T(8,128)S(1)} %copy-done.2), kind=kLoop, calls=%fused_computation.15 | loop fusion | flops 9437184 | bytes 8421888 | tf_op jit(solution)/shard_map/convert_element_type | solution.py:105
  160.9 4.1 %copy.12 = bf16[128,8192]{1,0:T(8,128)(2,1)} copy(bf16[128,8192]{0,1:T(8,128)(2,1)} %multiply_convert_fusion) | data formatting | bytes 4194304 | tf_op jit(solution)/shard_map/convert_element_type | solution.py:105
  (34 shorter events, 0.3 us)
Async XLA Ops:
  0.0 0.7 copy-start
  1.5 1.6 copy-start.5
  44.5 12.0 %copy-start.6 = (f32[64,2048]{1,0:T(8,128)S(1)}, f32[64,2048]{1,0:T(8,128)}, u32[]{:S(2)}) copy-start(f32[64,2048]{1,0:T(8,128)} %concatenate.13) | copy-start | bytes 1572868
  56.5 26.5 %dynamic-slice-start = ((f32[8192]{0:T(1024)}, s32[]{:T(128)}), f32[2048]{0:T(1024)S(1)}, s32[]{:S(2)}) async-start(f32[8192]{0:T(1024)} %param.12, s32[]{:T(128)} %select_n.32), calls=%async_computation.1 | async-start | bytes 16896 | tf_op jit(solution)/shard_map/dynamic_slice | solution.py:112
  62.2 10.8 %copy-start.3 = (f32[512,2048]{1,0:T(8,128)}, f32[512,2048]{1,0:T(8,128)S(1)}, u32[]{:S(2)}) copy-start(f32[512,2048]{1,0:T(8,128)S(1)} %get-tuple-element.170) | copy-start | bytes 12582916
  62.2 10.8 %copy-start.4 = (f32[512,2048]{1,0:T(8,128)}, f32[512,2048]{1,0:T(8,128)S(1)}, u32[]{:S(2)}) copy-start(f32[512,2048]{1,0:T(8,128)S(1)} %get-tuple-element.171) | copy-start | bytes 12582916
  89.4 53.7 %all-to-all-start = ((bf16[4,128,2048]{2,1,0:T(8,128)(2,1)}), bf16[4,128,2048]{2,1,0:T(8,128)(2,1)}, u32[]{:S(2)}, u32[]{:S(2)}) async-start(bf16[4,128,2048]{2,1,0:T(8,128)(2,1)} %pad_maximum_fusion), calls=%async_computation | async-start | bytes 4194304 | tf_op jit(solution)/shard_map/all_to_all | solution.py:115
  152.5 3.8 %copy-start.2 = (f32[128,4,2048]{0,2,1:T(8,128)S(1)}, f32[128,4,2048]{0,2,1:T(8,128)}, u32[]{:S(2)}) copy-start(f32[128,4,2048]{0,2,1:T(8,128)} %copy.10) | copy-start | bytes 12582916
  152.5 3.8 %copy-start.7 = (f32[8192]{0:T(1024)S(1)}, f32[8192]{0:T(1024)}, u32[]{:S(2)}) copy-start(f32[8192]{0:T(1024)} %param.13) | copy-start | bytes 98308
  156.3 8.6 %copy-start.1 = (bf16[512,16]{0,1:T(8,128)(2,1)S(1)}, bf16[512,16]{0,1:T(8,128)(2,1)}, u32[]{:S(2)}) copy-start(bf16[512,16]{0,1:T(8,128)(2,1)} %param.10) | copy-start | bytes 49156
